TPU v7x, 32 devices: a whole 2x2x4 slice. The times are simulated.
32 devices in a mesh: dp: 4 (over x, core), wide: 8 (over z, y).
Axes of the slice: x: 2, y: 2, z: 4, core: 2. Of those that a mesh axis runs over, the one named last changes fastest.
Arguments:
- streams: float32 [4, 4096, 2048], P(None, 'dp', 'wide'), may hold values from -8 to 8
- cotangent: float32 [4, 4096, 2048], P(None, 'dp', 'wide'), may hold values from -6 to 6
- w_query: bfloat16 [2048, 2048], P('dp', 'wide'), may hold values from -2 to 2
- w_key: bfloat16 [2048, 2048], P('dp', 'wide'), may hold values from -0.125 to 0.125
- w_value: bfloat16 [2048, 2048], P('dp', 'wide'), may hold values from -0.125 to 0.125
- w_out: bfloat16 [2048, 2048], P('wide', 'dp'), may hold values from -1 to 1
- w_gate: bfloat16 [2048, 8192], P('dp', 'wide'), may hold values from -0.125 to 0.125
- w_up: bfloat16 [2048, 8192], P('dp', 'wide'), may hold values from -0.125 to 0.125
- w_down: bfloat16 [8192, 2048], P('wide', 'dp'), may hold values from -0.0625 to 0.0625
- hyper: float32 [2, 4, 6], replicated, may hold values from 0.1 to 0.6
- doc_ids: int32 [4, 1024], P('dp'), may hold values from 0 to 3, never falling along the last dimension, each value on 1 to 512 neighbouring positions
- span_starts: int32 [4, 2], P('dp'), may hold values from 0 to 768, as said below
- span_lengths: int32 [4, 2], P('dp'), may hold values from 64 to 256
Outputs:
- out_streams: float32 [4, 4096, 2048], P(None, 'dp', 'wide')
- d_streams: float32 [4, 4096, 2048], P(None, 'dp', 'wide')
- grad_query: float32 [2048, 2048], P('dp', 'wide')
- grad_key: float32 [2048, 2048], P('dp', 'wide')
- grad_value: float32 [2048, 2048], P('dp', 'wide')
- grad_out: float32 [2048, 2048], P('wide', 'dp')
- grad_gate: float32 [2048, 8192], P('dp', 'wide')
- grad_up: float32 [2048, 8192], P('dp', 'wide')
- grad_down: float32 [8192, 2048], P('wide', 'dp')
- grad_hyper: float32 [2, 4, 6], replicated
- clip_scale: float32 [16], P('wide')
- query_clipped: float32 [2048, 2048], P('dp', 'wide')
- key_clipped: float32 [2048, 2048], P('dp', 'wide')
Inputs may be any that keep to these rules, and one draw needn't show every extreme that they name: `doc_ids`: each row's document numbers never fall; every document holds 1 to 512 tokens, and one holds exactly 512. `span_starts`: span k of a sequence starts and ends inside the k-th of 2 equal regions of the sequence.
All inputs are finite; a program needn't handle non-finite values.
Results may differ from a plain program's by a relative error of at most 0.018.
Values may be sent and summed in bfloat16 or wider, within the bound.
A program may use at most 192 MiB of HBM per device.

v0:
```python
import math
import jax
import jax.numpy as jnp
from jax import lax
from jax.sharding import PartitionSpec as P

D = 2048
H = 16
CLIP_TAU = 6
EPSILON = 1e-05
MASKED = -1e30


def rope_tables(length, head_size):
    half_size = head_size // 2
    inverse = 10000.0 ** (-2.0 * jnp.arange(half_size, dtype=jnp.float32) / head_size)
    angles = jnp.arange(length, dtype=jnp.float32)[:, None] * inverse[None, :]
    cosine_table = jnp.cos(angles)
    sine_table = jnp.sin(angles)
    return (
        jnp.concatenate([cosine_table, cosine_table], axis=1),
        jnp.concatenate([sine_table, sine_table], axis=1),
    )


def rotate(values, cosine_table, sine_table):
    half_size = values.shape[-1] // 2
    turned = jnp.concatenate([-values[..., half_size:], values[..., :half_size]], axis=-1)
    return values * cosine_table[:, None, :] + turned * sine_table[:, None, :]


def rotate_back(grads, cosine_table, sine_table):
    half_size = grads.shape[-1] // 2
    scaled = grads * sine_table[:, None, :]
    turned = jnp.concatenate([scaled[..., half_size:], -scaled[..., :half_size]], axis=-1)
    return grads * cosine_table[:, None, :] + turned


def mix_inputs(weights_in, stream_set):
    return jnp.sum(weights_in[:, None, None] * stream_set, axis=0)


def mix_streams(matrix, stream_set):
    return jnp.sum(matrix[:, :, None, None] * stream_set[None, :, :, :], axis=1)


def mix_back(matrix, grads):
    return jnp.sum(matrix[:, :, None, None] * grads[:, None, :, :], axis=0)


def hyper_rows(pre_grad, post_grad, mix_grad):
    return jnp.concatenate([pre_grad[:, None], post_grad[:, None], mix_grad], axis=1)


def span_labels(positions, starts, lengths):
    inside = (positions[:, None] >= starts[None, :]) & (
        positions[:, None] < (starts + lengths)[None, :]
    )
    numbers = jnp.arange(1, starts.shape[0] + 1, dtype=jnp.int32)
    return jnp.sum(jnp.where(inside, numbers[None, :], 0), axis=1)


def block_mask(doc_row, labels, start_row, count_rows):
    key_pos = jnp.arange(doc_row.shape[0], dtype=jnp.int32)
    query_pos = start_row + jnp.arange(count_rows, dtype=jnp.int32)
    query_docs = lax.dynamic_slice_in_dim(doc_row, start_row, count_rows)
    query_labels = lax.dynamic_slice_in_dim(labels, start_row, count_rows)
    same_doc = query_docs[:, None] == doc_row[None, :]
    causal = key_pos[None, :] <= query_pos[:, None]
    joint_span = (query_labels[:, None] > 0) & (query_labels[:, None] == labels[None, :])
    return same_doc & (causal | joint_span)


def attend_forward(queries, keys_roped, values, doc_row, starts, lengths, score_scale):
    length, head_count, head_size = queries.shape
    block_rows = min(512, length)
    labels = span_labels(jnp.arange(length, dtype=jnp.int32), starts, lengths)

    def one_block(block_index):
        start_row = block_index * block_rows
        query_rows = lax.dynamic_slice_in_dim(queries, start_row, block_rows, 0)
        scores = (
            jnp.einsum("qhd,khd->hqk", query_rows, keys_roped, preferred_element_type=jnp.float32)
            * score_scale
        )
        allowed = block_mask(doc_row, labels, start_row, block_rows)
        masked = jnp.where(allowed[None, :, :], scores, MASKED)
        largest = jnp.max(masked, axis=2)
        exponent = jnp.exp(masked - largest[:, :, None])
        totals = jnp.sum(exponent, axis=2)
        weights_low = (exponent / totals[:, :, None]).astype(jnp.bfloat16)
        attended = jnp.einsum(
            "hqk,khd->qhd", weights_low, values, preferred_element_type=jnp.float32
        )
        return (attended, largest + jnp.log(totals), jnp.max(largest, axis=1))

    attended, log_sums, block_tops = lax.map(
        one_block, jnp.arange(length // block_rows, dtype=jnp.int32)
    )
    return (attended.reshape(length, head_count, head_size), log_sums, jnp.max(block_tops, axis=0))


def attend_backward(
    queries, keys_roped, values, dout, log_sums, doc_row, starts, lengths, score_scale
):
    length, head_count, head_size = queries.shape
    block_rows = min(512, length)
    labels = span_labels(jnp.arange(length, dtype=jnp.int32), starts, lengths)

    def one_block(carry, inputs):
        key_grad, value_grad = carry
        block_index, log_rows = inputs
        start_row = block_index * block_rows
        query_rows = lax.dynamic_slice_in_dim(queries, start_row, block_rows, 0)
        dout_rows = lax.dynamic_slice_in_dim(dout, start_row, block_rows, 0)
        scores = (
            jnp.einsum("qhd,khd->hqk", query_rows, keys_roped, preferred_element_type=jnp.float32)
            * score_scale
        )
        allowed = block_mask(doc_row, labels, start_row, block_rows)
        masked = jnp.where(allowed[None, :, :], scores, MASKED)
        weights_full = jnp.where(allowed[None, :, :], jnp.exp(masked - log_rows[:, :, None]), 0.0)
        weight_grad = jnp.einsum(
            "qhd,khd->hqk", dout_rows, values, preferred_element_type=jnp.float32
        )
        centre = jnp.sum(weights_full * weight_grad, axis=2, keepdims=True)
        score_grad = (weights_full * (weight_grad - centre)).astype(jnp.bfloat16)
        query_grad = score_scale * jnp.einsum(
            "hqk,khd->qhd", score_grad, keys_roped, preferred_element_type=jnp.float32
        )
        key_grad = key_grad + score_scale * jnp.einsum(
            "hqk,qhd->khd", score_grad, query_rows, preferred_element_type=jnp.float32
        )
        value_grad = value_grad + jnp.einsum(
            "hqk,qhd->khd",
            weights_full.astype(jnp.bfloat16),
            dout_rows,
            preferred_element_type=jnp.float32,
        )
        return ((key_grad, value_grad), query_grad)

    empty_grad = jnp.zeros((length, head_count, head_size), jnp.float32)
    count_blocks = length // block_rows
    (key_grad, value_grad), query_grad = lax.scan(
        one_block, (empty_grad, empty_grad), (jnp.arange(count_blocks, dtype=jnp.int32), log_sums)
    )
    return (query_grad.reshape(length, head_count, head_size), key_grad, value_grad)


def row_sums(first_term, second_term):
    return lax.psum((jnp.sum(first_term, axis=1), jnp.sum(second_term, axis=1)), "wide")


def features(piece):
    return lax.all_gather(piece, "wide", axis=1, tiled=True)


def branch_rows(partial_value):
    return lax.psum_scatter(partial_value, "wide", scatter_dimension=1, tiled=True)


def norm_forward(hidden):
    local_width = hidden.shape[1]
    full_width = local_width * lax.axis_size("wide")
    row_total, squares = row_sums(hidden, hidden * hidden)
    centre = row_total / full_width
    spread = squares / full_width - centre * centre
    inverse = lax.rsqrt(spread + EPSILON)
    normed = (hidden - centre[:, None]) * inverse[:, None]
    return (features(normed.astype(jnp.bfloat16)), normed, inverse)


def norm_backward(partial_value, normed, inverse):
    full_width = partial_value.shape[1]
    grad_rows = lax.psum_scatter(partial_value, "wide", scatter_dimension=1, tiled=True)
    row_total, row_cross = row_sums(grad_rows, grad_rows * normed)
    return inverse[:, None] * (
        grad_rows - row_total[:, None] / full_width - normed * row_cross[:, None] / full_width
    )


def per_device(
    streams,
    cotangent,
    w_query,
    w_key,
    w_value,
    w_out,
    w_gate,
    w_up,
    w_down,
    hyper,
    doc_ids,
    span_starts,
    span_lengths,
):
    seq_count, length = doc_ids.shape
    tokens = streams.shape[1]
    head_size = D // H
    column_count = w_query.shape[1]
    head_count = column_count // head_size
    score_scale = 1.0 / math.sqrt(head_size)
    cosine_table, sine_table = rope_tables(length, head_size)
    shape_heads = (seq_count, length, head_count, head_size)
    attn_pre, attn_post, attn_mix = (hyper[0, :, 0], hyper[0, :, 1], hyper[0, :, 2:])
    ffn_pre, ffn_post, ffn_mix = (hyper[1, :, 0], hyper[1, :, 1], hyper[1, :, 2:])
    query_w, key_w, value_w, out_w = (
        lax.all_gather(w_query, "dp", axis=0, tiled=True),
        lax.all_gather(w_key, "dp", axis=0, tiled=True),
        lax.all_gather(w_value, "dp", axis=0, tiled=True),
        lax.all_gather(w_out, "dp", axis=1, tiled=True),
    )
    gate_w, up_w, down_w = (
        lax.all_gather(w_gate, "dp", axis=0, tiled=True),
        lax.all_gather(w_up, "dp", axis=0, tiled=True),
        lax.all_gather(w_down, "dp", axis=1, tiled=True),
    )
    normed_one, kept_one, inverse_one = norm_forward(mix_inputs(attn_pre, streams))
    query_raw = jnp.dot(normed_one, query_w, preferred_element_type=jnp.float32).reshape(
        shape_heads
    )
    key_raw = jnp.dot(normed_one, key_w, preferred_element_type=jnp.float32).reshape(shape_heads)
    values = (
        jnp.dot(normed_one, value_w, preferred_element_type=jnp.float32)
        .astype(jnp.bfloat16)
        .reshape(shape_heads)
    )
    queries = rotate(query_raw, cosine_table, sine_table).astype(jnp.bfloat16)
    keys_roped = rotate(key_raw, cosine_table, sine_table).astype(jnp.bfloat16)

    def forward_sequence(inputs):
        return attend_forward(
            inputs[0], inputs[1], inputs[2], inputs[3], inputs[4], inputs[5], score_scale
        )

    attended, log_sums, seq_tops = lax.map(
        forward_sequence, (queries, keys_roped, values, doc_ids, span_starts, span_lengths)
    )
    head_top = lax.pmax(jnp.max(seq_tops, axis=0), "dp")
    attended_low = attended.reshape(tokens, column_count).astype(jnp.bfloat16)
    branch_one = branch_rows(jnp.dot(attended_low, out_w, preferred_element_type=jnp.float32))
    after_attn = mix_streams(attn_mix, streams) + attn_post[:, None, None] * branch_one[None, :, :]
    normed_two, kept_two, inverse_two = norm_forward(mix_inputs(ffn_pre, after_attn))
    gate_proj = jnp.dot(normed_two, gate_w, preferred_element_type=jnp.float32)
    up_proj = jnp.dot(normed_two, up_w, preferred_element_type=jnp.float32)
    sigmoid_gate = jax.nn.sigmoid(gate_proj)
    hidden = (gate_proj * sigmoid_gate * up_proj).astype(jnp.bfloat16)
    branch_two = branch_rows(jnp.dot(hidden, down_w, preferred_element_type=jnp.float32))
    out_streams = (
        mix_streams(ffn_mix, after_attn) + ffn_post[:, None, None] * branch_two[None, :, :]
    )
    ffn_post_grad = jnp.sum(cotangent * branch_two[None, :, :], axis=(1, 2))
    ffn_mix_grad = jnp.sum(cotangent[:, None, :, :] * after_attn[None, :, :, :], axis=(2, 3))
    two_grad = features(jnp.sum(ffn_post[:, None, None] * cotangent, axis=0).astype(jnp.bfloat16))
    hidden_grad = jnp.dot(two_grad, down_w.T, preferred_element_type=jnp.float32)
    down_wgrad = jnp.einsum("tf,td->fd", hidden, two_grad, preferred_element_type=jnp.float32)
    gate_grad = (
        hidden_grad * up_proj * sigmoid_gate * (1.0 + gate_proj * (1.0 - sigmoid_gate))
    ).astype(jnp.bfloat16)
    up_grad = (hidden_grad * gate_proj * sigmoid_gate).astype(jnp.bfloat16)
    gate_wgrad = jnp.einsum("td,tf->df", normed_two, gate_grad, preferred_element_type=jnp.float32)
    up_wgrad = jnp.einsum("td,tf->df", normed_two, up_grad, preferred_element_type=jnp.float32)
    gate_shard, up_shard, down_shard = (
        lax.psum_scatter(gate_wgrad, "dp", scatter_dimension=0, tiled=True),
        lax.psum_scatter(up_wgrad, "dp", scatter_dimension=0, tiled=True),
        lax.psum_scatter(down_wgrad, "dp", scatter_dimension=1, tiled=True),
    )
    normed_two_grad = jnp.dot(gate_grad, gate_w.T, preferred_element_type=jnp.float32) + jnp.dot(
        up_grad, up_w.T, preferred_element_type=jnp.float32
    )
    h_two_grad = norm_backward(normed_two_grad, kept_two, inverse_two)
    ffn_pre_grad = jnp.sum(h_two_grad[None, :, :] * after_attn, axis=(1, 2))
    after_grad = mix_back(ffn_mix, cotangent) + ffn_pre[:, None, None] * h_two_grad[None, :, :]
    attn_post_grad = jnp.sum(after_grad * branch_one[None, :, :], axis=(1, 2))
    attn_mix_grad = jnp.sum(after_grad[:, None, :, :] * streams[None, :, :, :], axis=(2, 3))
    one_grad = features(jnp.sum(attn_post[:, None, None] * after_grad, axis=0).astype(jnp.bfloat16))
    attended_grad = jnp.dot(one_grad, out_w.T, preferred_element_type=jnp.float32).astype(
        jnp.bfloat16
    )
    out_wgrad = jnp.einsum("tc,td->cd", attended_low, one_grad, preferred_element_type=jnp.float32)

    def backward_sequence(inputs):
        return attend_backward(
            inputs[0],
            inputs[1],
            inputs[2],
            inputs[3],
            inputs[4],
            inputs[5],
            inputs[6],
            inputs[7],
            score_scale,
        )

    query_grad, key_grad, value_grad = lax.map(
        backward_sequence,
        (
            queries,
            keys_roped,
            values,
            attended_grad.reshape(shape_heads),
            log_sums,
            doc_ids,
            span_starts,
            span_lengths,
        ),
    )
    query_low = (
        rotate_back(query_grad, cosine_table, sine_table)
        .reshape(tokens, column_count)
        .astype(jnp.bfloat16)
    )
    key_low = (
        rotate_back(key_grad, cosine_table, sine_table)
        .reshape(tokens, column_count)
        .astype(jnp.bfloat16)
    )
    value_low = value_grad.reshape(tokens, column_count).astype(jnp.bfloat16)
    query_wgrad = jnp.einsum("td,tc->dc", normed_one, query_low, preferred_element_type=jnp.float32)
    key_wgrad = jnp.einsum("td,tc->dc", normed_one, key_low, preferred_element_type=jnp.float32)
    value_wgrad = jnp.einsum("td,tc->dc", normed_one, value_low, preferred_element_type=jnp.float32)
    normed_one_grad = (
        jnp.dot(query_low, query_w.T, preferred_element_type=jnp.float32)
        + jnp.dot(key_low, key_w.T, preferred_element_type=jnp.float32)
        + jnp.dot(value_low, value_w.T, preferred_element_type=jnp.float32)
    )
    h_one_grad = norm_backward(normed_one_grad, kept_one, inverse_one)
    attn_pre_grad = jnp.sum(h_one_grad[None, :, :] * streams, axis=(1, 2))
    streams_grad = mix_back(attn_mix, after_grad) + attn_pre[:, None, None] * h_one_grad[None, :, :]
    hyper_grad = lax.psum(
        jnp.stack(
            [
                hyper_rows(attn_pre_grad, attn_post_grad, attn_mix_grad),
                hyper_rows(ffn_pre_grad, ffn_post_grad, ffn_mix_grad),
            ]
        ),
        ("dp", "wide"),
    )
    query_shard, key_shard, value_shard, out_shard = (
        lax.psum_scatter(query_wgrad, "dp", scatter_dimension=0, tiled=True),
        lax.psum_scatter(key_wgrad, "dp", scatter_dimension=0, tiled=True),
        lax.psum_scatter(value_wgrad, "dp", scatter_dimension=0, tiled=True),
        lax.psum_scatter(out_wgrad, "dp", scatter_dimension=1, tiled=True),
    )
    clip_scale = jnp.sqrt(CLIP_TAU / jnp.maximum(head_top, CLIP_TAU))
    columns = jnp.repeat(clip_scale, head_size)[None, :]
    return (
        out_streams,
        streams_grad,
        query_shard,
        key_shard,
        value_shard,
        out_shard,
        gate_shard,
        up_shard,
        down_shard,
        hyper_grad,
        clip_scale,
        w_query.astype(jnp.float32) * columns,
        w_key.astype(jnp.float32) * columns,
    )


def solution(mesh):
    return jax.shard_map(
        per_device,
        mesh=mesh,
        in_specs=(
            P(None, "dp", "wide"),
            P(None, "dp", "wide"),
            P("dp", "wide"),
            P("dp", "wide"),
            P("dp", "wide"),
            P("wide", "dp"),
            P("dp", "wide"),
            P("dp", "wide"),
            P("wide", "dp"),
            P(),
            P("dp", None),
            P("dp", None),
            P("dp", None),
        ),
        out_specs=(
            P(None, "dp", "wide"),
            P(None, "dp", "wide"),
            P("dp", "wide"),
            P("dp", "wide"),
            P("dp", "wide"),
            P("wide", "dp"),
            P("dp", "wide"),
            P("dp", "wide"),
            P("wide", "dp"),
            P(),
            P("wide"),
            P("dp", "wide"),
            P("dp", "wide"),
        ),
        check_vma=False,
    )
```

profile of v0, /device:TPU:0, one launch (start us, length us, event | category | flops | bytes accessed | tf_op | source)
XLA Modules:
  0.0 1579.7 jit_solution(8456090871075567823)
XLA Ops:
  11.9 23.4 %all-reduce.3 = (f32[1024]{0:T(1024)S(1)}, f32[1024]{0:T(1024)S(1)}) all-reduce(f32[1024]{0:T(1024)S(1)} %multiply_reduce_fusion.20, f32[1024]{0:T(1024)S(1)} %get-tuple-element.312), channel_id=1, replica_groups=mesh['dp'=4,'wide'=8] {'wide'}, use_global_device_ids=true, to_apply=%region_5.6 | all-reduce | flops 2048 | bytes 16384 | tf_op jit(solution)/shard_map/psum | solution.py:151
  42.8 66.4 %all-gather.12.cloned.1.call-done = bf16[1024,2048]{1,0:T(8,128)(2,1)} async-done(((bf16[1024,256]{1,0:T(8,128)(2,1)}), bf16[1024,2048]{1,0:T(8,128)(2,1)}) %all-gather.12.cloned.1.call-update) | async-done | bytes 4194320 | tf_op jit(solution)/shard_map/all_gather | solution.py:155
  147.9 14.2 while.53
  175.5 141.2 %reduce-scatter.12.cloned.1.call-done = f32[1024,256]{1,0:T(8,128)} async-done(((f32[1024,2048]{1,0:T(8,128)}), f32[1024,256]{1,0:T(8,128)}) %reduce-scatter.12.cloned.1.call-update) | async-done | bytes 1048592 | tf_op jit(solution)/shard_map/reduce_scatter | solution.py:159
  322.2 19.7 %all-reduce.2 = (f32[1024]{0:T(1024)S(1)}, f32[1024]{0:T(1024)S(1)}) all-reduce(f32[1024]{0:T(1024)S(1)} %multiply_reduce_fusion.19, f32[1024]{0:T(1024)S(1)} %get-tuple-element.310), channel_id=1, replica_groups=mesh['dp'=4,'wide'=8] {'wide'}, use_global_device_ids=true, to_apply=%region_18.19 | all-reduce | flops 2048 | bytes 16384 | tf_op jit(solution)/shard_map/psum | solution.py:151
  351.8 77.3 %all-gather.22.cloned.1.call-done = bf16[1024,2048]{1,0:T(8,128)(2,1)} async-done(((bf16[1024,256]{1,0:T(8,128)(2,1)}), bf16[1024,2048]{1,0:T(8,128)(2,1)}) %all-gather.22.cloned.1.call-update) | async-done | bytes 4194320 | tf_op jit(solution)/shard_map/all_gather | solution.py:155
  439.1 24.3 %all-gather.26.cloned.1.call-done = bf16[2048,1024]{1,0:T(8,128)(2,1)} async-done(((bf16[512,1024]{1,0:T(8,128)(2,1)}), bf16[2048,1024]{1,0:T(8,128)(2,1)}) %all-gather.26.cloned.1.call-update) | async-done | bytes 4194320 | tf_op jit(solution)/shard_map/all_gather | solution.py:215
  475.4 23.8 %all-gather.28.cloned.1.call-done = bf16[1024,2048]{1,0:T(8,128)(2,1)} async-done(((bf16[1024,512]{1,0:T(8,128)(2,1)}), bf16[1024,2048]{1,0:T(8,128)(2,1)}) %all-gather.28.cloned.1.call-update) | async-done | bytes 4194320 | tf_op jit(solution)/shard_map/all_gather | solution.py:216
  520.7 137.2 %reduce-scatter.14.cloned.1.call-done = f32[1024,256]{1,0:T(8,128)} async-done(((f32[1024,2048]{1,0:T(8,128)}), f32[1024,256]{1,0:T(8,128)}) %reduce-scatter.14.cloned.1.call-update) | async-done | bytes 1048592 | tf_op jit(solution)/shard_map/reduce_scatter | solution.py:159
  666.3 73.4 %all-gather.30.cloned.1.call-done = bf16[1024,2048]{1,0:T(8,128)(2,1)} async-done(((bf16[1024,256]{1,0:T(8,128)(2,1)}), bf16[1024,2048]{1,0:T(8,128)(2,1)}) %all-gather.30.cloned.1.call-update) | async-done | bytes 4194320 | tf_op jit(solution)/shard_map/all_gather | solution.py:155
  739.7 12.9 multiply_convert_fusion.1
  766.6 146.1 %reduce-scatter.16.cloned.1.call-done = f32[1024,256]{1,0:T(8,128)} async-done(((f32[1024,2048]{1,0:T(8,128)}), f32[1024,256]{1,0:T(8,128)}) %reduce-scatter.16.cloned.1.call-update) | async-done | bytes 1048592 | tf_op jit(solution)/shard_map/reduce_scatter | solution.py:175
  914.6 19.9 %all-reduce.1 = (f32[1024]{0:T(1024)S(1)}, f32[1024]{0:T(1024)S(1)}) all-reduce(f32[1024]{0:T(1024)S(1)} %get-tuple-element.326, f32[1024]{0:T(1024)S(1)} %get-tuple-element.325), channel_id=1, replica_groups=mesh['dp'=4,'wide'=8] {'wide'}, use_global_device_ids=true, to_apply=%region_26.27 | all-reduce | flops 2048 | bytes 16384 | tf_op jit(solution)/shard_map/psum | solution.py:151
  948.7 68.3 %all-gather.32.cloned.1.call-done = bf16[1024,2048]{1,0:T(8,128)(2,1)} async-done(((bf16[1024,256]{1,0:T(8,128)(2,1)}), bf16[1024,2048]{1,0:T(8,128)(2,1)}) %all-gather.32.cloned.1.call-update) | async-done | bytes 4194320 | tf_op jit(solution)/shard_map/all_gather | solution.py:155
  1020.7 30.5 %while.54 = (s32[]{:T(128)}, f32[1024,2,128]{0,2,1:T(8,128)S(1)}, f32[1024,2,128]{0,2,1:T(8,128)}, f32[2,512,2,128]{3,1,2,0:T(8,128)}, s32[2]{0:T(128)S(1)}, /*i...) while((s32[]{:T(128)}, f32[1024,2,128]{0,2,1:T(8,128)S(1)}, ...), condition=%wide.region_31.32_spmd.clone.clone, body=%wide.region_29.31_spmd.clone.sunk.clone | while | flops 1357250560 | bytes 90224648 | solution.py:144
  1135.9 76.0 %reduce-scatter.18.cloned.1.call-done = f32[1024,256]{1,0:T(8,128)} async-done(((f32[1024,2048]{1,0:T(8,128)}), f32[1024,256]{1,0:T(8,128)}) %reduce-scatter.18.cloned.1.call-update) | async-done | bytes 1048592 | tf_op jit(solution)/shard_map/reduce_scatter | solution.py:175
  1213.8 19.7 %all-reduce = (f32[1024]{0:T(1024)S(1)}, f32[1024]{0:T(1024)S(1)}) all-reduce(f32[1024]{0:T(1024)S(1)} %get-tuple-element.324, f32[1024]{0:T(1024)S(1)} %get-tuple-element.323), channel_id=1, replica_groups=mesh['dp'=4,'wide'=8] {'wide'}, use_global_device_ids=true, to_apply=%region_36.37 | all-reduce | flops 2048 | bytes 16384 | tf_op jit(solution)/shard_map/psum | solution.py:151
  1242.9 38.0 %psum.71 = f32[2,4,6]{2,1,0:T(4,128)} all-reduce(f32[2,4,6]{2,1,0:T(4,128)S(1)} %pad_maximum_fusion.3), channel_id=1, replica_groups=mesh['dp'=4,'wide'=8] {'dp','wide'}, use_global_device_ids=true, to_apply=%region_50.51 | all-reduce | flops 48 | bytes 384 | tf_op jit(solution)/shard_map/psum | solution.py:330
  1286.7 74.4 %reduce-scatter.28.cloned.1.call-done = f32[512,1024]{1,0:T(8,128)} async-done(((f32[2048,1024]{1,0:T(8,128)}), f32[512,1024]{1,0:T(8,128)}) %reduce-scatter.28.cloned.1.call-update) | async-done | bytes 2097168 | tf_op jit(solution)/shard_map/reduce_scatter | solution.py:264
  1361.1 74.4 %reduce-scatter.30.cloned.1.call-done = f32[512,1024]{1,0:T(8,128)} async-done(((f32[2048,1024]{1,0:T(8,128)}), f32[512,1024]{1,0:T(8,128)}) %reduce-scatter.30.cloned.1.call-update) | async-done | bytes 2097168 | tf_op jit(solution)/shard_map/reduce_scatter | solution.py:265
  1435.6 34.3 %reduce-scatter.22.cloned.1.call-done = f32[512,256]{1,0:T(8,128)} async-done(((f32[2048,256]{1,0:T(8,128)}), f32[512,256]{1,0:T(8,128)}) %reduce-scatter.22.cloned.1.call-update) | async-done | bytes 524304 | tf_op jit(solution)/shard_map/reduce_scatter | solution.py:341
  1469.9 34.2 %reduce-scatter.20.cloned.1.call-done = f32[512,256]{1,0:T(8,128)} async-done(((f32[2048,256]{1,0:T(8,128)}), f32[512,256]{1,0:T(8,128)}) %reduce-scatter.20.cloned.1.call-update) | async-done | bytes 524304 | tf_op jit(solution)/shard_map/reduce_scatter | solution.py:340
  1504.0 34.3 %reduce-scatter.26.cloned.1.call-done = f32[256,512]{1,0:T(8,128)} async-done(((f32[256,2048]{1,0:T(8,128)}), f32[256,512]{1,0:T(8,128)}) %reduce-scatter.26.cloned.1.call-update) | async-done | bytes 524304 | tf_op jit(solution)/shard_map/reduce_scatter | solution.py:343
  1538.4 34.3 %reduce-scatter.24.cloned.1.call-done = f32[512,256]{1,0:T(8,128)} async-done(((f32[2048,256]{1,0:T(8,128)}), f32[512,256]{1,0:T(8,128)}) %reduce-scatter.24.cloned.1.call-update) | async-done | bytes 524304 | tf_op jit(solution)/shard_map/reduce_scatter | solution.py:342
  (302 shorter events, 307.1 us)
Async XLA Ops:
  7.2 35.6 %all-gather.16.cloned.1.call-start = ((), (), s32[]{:S(2)}) async-start(), calls=%async_computation.13 | async-start | bytes 1310720 | tf_op jit(solution)/shard_map/all_gather | solution.py:209
  7.9 101.3 %all-gather.12.cloned.1.call-start = ((), (), s32[]{:S(2)}) async-start(), calls=%async_computation.11 | async-start | bytes 4718592 | tf_op jit(solution)/shard_map/all_gather | solution.py:155
  37.1 88.5 %all-gather.14.cloned.1.call-start = ((), (), s32[]{:S(2)}) async-start(), calls=%async_computation.12 | async-start | bytes 1310720 | tf_op jit(solution)/shard_map/all_gather | solution.py:208
  37.9 105.9 %all-gather.18.cloned.1.call-start = ((), (), s32[]{:S(2)}) async-start(), calls=%async_computation.14 | async-start | bytes 1310720 | tf_op jit(solution)/shard_map/all_gather | solution.py:210
  38.5 124.3 %all-gather.20.cloned.1.call-start = ((), (), s32[]{:S(2)}) async-start(), calls=%async_computation.15 | async-start | bytes 1310720 | tf_op jit(solution)/shard_map/all_gather | solution.py:211
  39.0 277.6 %reduce-scatter.12.cloned.1.call-start = ((), (), s32[]{:S(2)}) async-start(), calls=%async_computation.16 | async-start | bytes 9437184 | tf_op jit(solution)/shard_map/reduce_scatter | solution.py:159
  42.5 902.6 %copy-start.12 = (f32[1024,128]{0,1:T(8,128)}, f32[1024,128]{0,1:T(8,128)S(1)}, u32[]{:S(2)}) copy-start(f32[1024,128]{0,1:T(8,128)S(1)} %copy.61) | copy-start | bytes 1572868
  168.6 183.2 %all-gather.24.cloned.1.call-start = ((), (), s32[]{:S(2)}) async-start(), calls=%async_computation.18 | async-start | bytes 5242880 | tf_op jit(solution)/shard_map/all_gather | solution.py:214
  169.4 259.7 %all-gather.22.cloned.1.call-start = ((), (), s32[]{:S(2)}) async-start(), calls=%async_computation.17 | async-start | bytes 4718592 | tf_op jit(solution)/shard_map/all_gather | solution.py:155
  343.1 120.2 %all-gather.26.cloned.1.call-start = ((), (), s32[]{:S(2)}) async-start(), calls=%async_computation.19 | async-start | bytes 5242880 | tf_op jit(solution)/shard_map/all_gather | solution.py:215
  343.8 155.4 %all-gather.28.cloned.1.call-start = ((), (), s32[]{:S(2)}) async-start(), calls=%async_computation.20 | async-start | bytes 5242880 | tf_op jit(solution)/shard_map/all_gather | solution.py:216
  344.4 313.4 %reduce-scatter.14.cloned.1.call-start = ((), (), s32[]{:S(2)}) async-start(), calls=%async_computation.21 | async-start | bytes 9437184 | tf_op jit(solution)/shard_map/reduce_scatter | solution.py:159
  509.8 229.9 %all-gather.30.cloned.1.call-start = ((), (), s32[]{:S(2)}) async-start(), calls=%async_computation.22 | async-start | bytes 4718592 | tf_op jit(solution)/shard_map/all_gather | solution.py:155
  665.9 246.9 %reduce-scatter.16.cloned.1.call-start = ((), (), s32[]{:S(2)}) async-start(), calls=%async_computation.23 | async-start | bytes 9437184 | tf_op jit(solution)/shard_map/reduce_scatter | solution.py:175
  766.6 250.4 %all-gather.32.cloned.1.call-start = ((), (), s32[]{:S(2)}) async-start(), calls=%async_computation.24 | async-start | bytes 4718592 | tf_op jit(solution)/shard_map/all_gather | solution.py:155
  944.9 267.0 %reduce-scatter.18.cloned.1.call-start = ((), (), s32[]{:S(2)}) async-start(), calls=%async_computation.25 | async-start | bytes 9437184 | tf_op jit(solution)/shard_map/reduce_scatter | solution.py:175
  1065.7 221.0 %reduce-scatter.32.cloned.1.call-start = ((), (), s32[]{:S(2)}) async-start(), calls=%async_computation.32 | async-start | bytes 10485760 | tf_op jit(solution)/shard_map/reduce_scatter | solution.py:266
  1076.6 284.5 %reduce-scatter.28.cloned.1.call-start = ((), (), s32[]{:S(2)}) async-start(), calls=%async_computation.30 | async-start | bytes 10485760 | tf_op jit(solution)/shard_map/reduce_scatter | solution.py:264
  1087.4 348.2 %reduce-scatter.30.cloned.1.call-start = ((), (), s32[]{:S(2)}) async-start(), calls=%async_computation.31 | async-start | bytes 10485760 | tf_op jit(solution)/shard_map/reduce_scatter | solution.py:265
  1098.6 371.3 %reduce-scatter.22.cloned.1.call-start = ((), (), s32[]{:S(2)}) async-start(), calls=%async_computation.27 | async-start | bytes 2621440 | tf_op jit(solution)/shard_map/reduce_scatter | solution.py:341
  1103.5 400.5 %reduce-scatter.20.cloned.1.call-start = ((), (), s32[]{:S(2)}) async-start(), calls=%async_computation.26 | async-start | bytes 2621440 | tf_op jit(solution)/shard_map/reduce_scatter | solution.py:340
  1108.6 429.7 %reduce-scatter.26.cloned.1.call-start = ((), (), s32[]{:S(2)}) async-start(), calls=%async_computation.29 | async-start | bytes 2621440 | tf_op jit(solution)/shard_map/reduce_scatter | solution.py:343
  1113.9 458.8 %reduce-scatter.24.cloned.1.call-start = ((), (), s32[]{:S(2)}) async-start(), calls=%async_computation.28 | async-start | bytes 2621440 | tf_op jit(solution)/shard_map/reduce_scatter | solution.py:342
  1135.9 99.5 %copy-start.39 = (f32[4]{0:T(128)S(1)}, f32[4]{0:T(128)}, u32[]{:S(2)}) copy-start(f32[4]{0:T(128)} %copy-done.38) | copy-start | bytes 52
  (57 other events, 722.8 us)
Sparse Core Ops, SparseCore 0:
  9.5 19.4 all-gather.15
  37.3 71.8 all-gather.11
  110.8 14.8 all-gather.13
  127.1 16.6 all-gather.17
  145.2 16.6 all-gather.19
  168.7 147.8 reduce-scatter.11
  318.2 33.5 all-gather.23
  354.4 74.6 all-gather.21
  430.7 32.6 all-gather.25
  464.7 34.4 all-gather.27
  509.9 147.8 reduce-scatter.13
  666.0 73.7 all-gather.29
  766.7 146.0 reduce-scatter.15
  945.1 71.8 all-gather.31
  1065.9 146.0 reduce-scatter.17
  1214.9 71.7 reduce-scatter.31
  1289.7 71.3 reduce-scatter.27
  1364.1 71.3 reduce-scatter.29
  1438.7 31.1 reduce-scatter.21
  1472.8 31.1 reduce-scatter.19
  1507.2 31.1 reduce-scatter.25
  1541.5 31.1 reduce-scatter.23
where the time goes:
time: 1590 us; the launch traced here: 1580 us
  waiting for transfers between devices  1160 us (73%)
  matrix products  165 us (10%)
  blocking collectives  127 us (8%)
  other arithmetic  86.2 us (5%)
  local copies, waits for them, and re-layouts  21 us (1%)
    all_gather x4, waiting for transfers between devices, features(): return lax.all_gather(piece, 'wide', axis=1, tiled=True)  285 us
    reduce_scatter x2, waiting for transfers between devices, branch_rows(): lax.psum_scatter(partial_value, 'wide', scatter_dimension=1, tiled=True)  278 us
    reduce_scatter x2, waiting for transfers between devices, norm_backward(): lax.psum_scatter(partial_value, 'wide', scatter_dimension=1, tiled=True)  222 us
    psum x4, blocking collectives, row_sums(): lax.psum((jnp.sum(first_term, axis=1), jnp.sum(second_term, axis=1)), 'wi...  82.8 us
    reduce_scatter x1, waiting for transfers between devices, per_device(): lax.psum_scatter(up_wgrad, 'dp', scatter_dimension=0, tiled=True)  74.4 us
    reduce_scatter x1, waiting for transfers between devices, per_device(): lax.psum_scatter(gate_wgrad, 'dp', scatter_dimension=0, tiled=True)  74.4 us
    psum x1, blocking collectives, per_device(): lax.psum(jnp.stack([hyper_rows(attn_pre_grad, attn_post_grad, attn_mix_gr...  38 us
    reduce_scatter x1, waiting for transfers between devices, per_device(): lax.psum_scatter(out_wgrad, 'dp', scatter_dimension=1, tiled=True)  34.3 us
  transfers between devices with their start and end apart: 22, of which 20 were waited for; matrix products, arithmetic and copies ran while one was open for 10% of the time, Pallas kernels for 0%

commit v1 on v0

--- a/solution.py
+++ b/solution.py
@@ -9,6 +9,22 @@
 CLIP_TAU = 6
 EPSILON = 1e-05
 MASKED = -1e30
+
+
+def collect(x, axis, dim):
+    ways, here, lap = (lax.axis_size(axis), lax.axis_index(axis), x.shape[dim])
+    lengths = [n * ways if d == dim else n for d, n in enumerate(x.shape)]
+    full = lax.dynamic_update_slice_in_dim(jnp.zeros(lengths, x.dtype), x, here * lap, axis=dim)
+    going_up = going_down = x
+    for far in range(1, ways // 2 + 1):
+        going_up = lax.ppermute(going_up, axis, [(d, (d + 1) % ways) for d in range(ways)])
+        full = lax.dynamic_update_slice_in_dim(full, going_up, (here - far) % ways * lap, axis=dim)
+        if 2 * far < ways:
+            going_down = lax.ppermute(going_down, axis, [(d, (d - 1) % ways) for d in range(ways)])
+            full = lax.dynamic_update_slice_in_dim(
+                full, going_down, (here + far) % ways * lap, axis=dim
+            )
+    return full
 
 
 def rope_tables(length, head_size):
@@ -152,7 +168,7 @@
 
 
 def features(piece):
-    return lax.all_gather(piece, "wide", axis=1, tiled=True)
+    return collect(piece, "wide", 1)
 
 
 def branch_rows(partial_value):

time: 1590 us -> 1540 us (0.969)
  waiting for transfers between devices: 1160 us -> 1020 us
  starting transfers between devices: 2.09 us -> 77.3 us
  local copies, waits for them, and re-layouts: 21 us -> 46.7 us
    all_gather x4 -> x0, waiting for transfers between devices: 285 us -> none  [features(): return lax.all_gather(piece, 'wide', axis=1, tiled=True)]
    ppermute x0 -> x28, waiting for transfers between devices: none -> 233 us  [the longest x16 233 us: collect(): lax.ppermute(going_up, axis, [(d, (d + 1) % ways) for d in range(ways)])]
    ppermute x0 -> x28, starting transfers between devices: none -> 75.6 us  [the longest x12 43.5 us: collect(): lax.ppermute(going_down, axis, [(d, (d - 1) % ways) for d in range(ways)])]
    all_gather x1, waiting for transfers between devices: 24.3 us -> 0.01 us  [per_device(): lax.all_gather(w_up, 'dp', axis=0, tiled=True)]
    all_gather x1, waiting for transfers between devices: 23.8 us -> 0.01 us  [per_device(): lax.all_gather(w_down, 'dp', axis=1, tiled=True)]
    dynamic_update_slice x0 -> x30, local copies, waits for them, and re-layouts: none -> 19.1 us  [the longest x16 10.4 us: collect(): lax.dynamic_update_slice_in_dim(full, going_up, (here - far) % ways * lap...]
  transfers between devices with their start and end apart: 22 -> 46, of which waited for: 20 -> 27; matrix products, arithmetic and copies ran while one was open for 10% -> 12% of each run, Pallas kernels for 0% -> 0%
where the time goes in v1:
time: 1540 us; the launch traced here: 1530 us
  waiting for transfers between devices  1020 us (66%)
  matrix products  160 us (10%)
  blocking collectives  127 us (8%)
  other arithmetic  84.9 us (6%)
  starting transfers between devices  77.3 us (5%)
  local copies, waits for them, and re-layouts  46.7 us (3%)
  between operations  15.8 us (1%)
    reduce_scatter x2, waiting for transfers between devices, branch_rows(): lax.psum_scatter(partial_value, 'wide', scatter_dimension=1, tiled=True)  270 us
    ppermute x16, waiting for transfers between devices, collect(): lax.ppermute(going_up, axis, [(d, (d + 1) % ways) for d in range(ways)])  233 us
    reduce_scatter x2, waiting for transfers between devices, norm_backward(): lax.psum_scatter(partial_value, 'wide', scatter_dimension=1, tiled=True)  220 us
    psum x4, blocking collectives, row_sums(): lax.psum((jnp.sum(first_term, axis=1), jnp.sum(second_term, axis=1)), 'wi...  82.6 us
    reduce_scatter x1, waiting for transfers between devices, per_device(): lax.psum_scatter(gate_wgrad, 'dp', scatter_dimension=0, tiled=True)  74.6 us
    reduce_scatter x1, waiting for transfers between devices, per_device(): lax.psum_scatter(up_wgrad, 'dp', scatter_dimension=0, tiled=True)  74.4 us
    ppermute x12, starting transfers between devices, collect(): lax.ppermute(going_down, axis, [(d, (d - 1) % ways) for d in range(ways)])  43.5 us
    psum x1, blocking collectives, per_device(): lax.psum(jnp.stack([hyper_rows(attn_pre_grad, attn_post_grad, attn_mix_gr...  38 us
  transfers between devices with their start and end apart: 46, of which 27 were waited for; matrix products, arithmetic and copies ran while one was open for 12% of the time, Pallas kernels for 0%

profile of v1, /device:TPU:0, one launch (start us, length us, event | category | flops | bytes accessed | tf_op | source)
XLA Modules:
  0.0 1533.5 jit_solution(16126795838207256441)
XLA Ops:
  13.5 23.4 %all-reduce.3 = (f32[1024]{0:T(1024)S(1)}, f32[1024]{0:T(1024)S(1)}) all-reduce(f32[1024]{0:T(1024)S(1)} %multiply_reduce_fusion.20, f32[1024]{0:T(1024)S(1)} %get-tuple-element.312), channel_id=1, replica_groups=mesh['dp'=4,'wide'=8] {'wide'}, use_global_device_ids=true, to_apply=%region_5.6 | all-reduce | flops 2048 | bytes 16384 | tf_op jit(solution)/shard_map/psum | solution.py:167
  67.8 16.3 %collective-permute-done.2 = bf16[1024,256]{1,0:T(8,128)(2,1)S(1)} collective-permute-done((bf16[1024,256]{1,0:T(8,128)(2,1)S(1)}, bf16[1024,256]{1,0:T(8,128)(2,1)S(1)}, u32[]{:S(2)}, u32[]{:S(2)}) %collective-permute-start.2) | collective-permute-done | bytes 524320 | tf_op jit(solution)/shard_map/ppermute | solution.py:20
  92.0 15.8 %collective-permute-done.4 = bf16[1024,256]{1,0:T(8,128)(2,1)} collective-permute-done((bf16[1024,256]{1,0:T(8,128)(2,1)S(1)}, bf16[1024,256]{1,0:T(8,128)(2,1)}, u32[]{:S(2)}, u32[]{:S(2)}) %collective-permute-start.4) | collective-permute-done | bytes 524320 | tf_op jit(solution)/shard_map/ppermute | solution.py:20
  167.0 136.1 %reduce-scatter.12.cloned.1.call-done = f32[1024,256]{1,0:T(8,128)} async-done(((f32[1024,2048]{1,0:T(8,128)}), f32[1024,256]{1,0:T(8,128)}) %reduce-scatter.12.cloned.1.call-update) | async-done | bytes 1048592 | tf_op jit(solution)/shard_map/reduce_scatter | solution.py:175
  308.6 19.7 %all-reduce.2 = (f32[1024]{0:T(1024)S(1)}, f32[1024]{0:T(1024)S(1)}) all-reduce(f32[1024]{0:T(1024)S(1)} %multiply_reduce_fusion.19, f32[1024]{0:T(1024)S(1)} %get-tuple-element.310), channel_id=1, replica_groups=mesh['dp'=4,'wide'=8] {'wide'}, use_global_device_ids=true, to_apply=%region_18.19 | all-reduce | flops 2048 | bytes 16384 | tf_op jit(solution)/shard_map/psum | solution.py:167
  358.2 17.3 %collective-permute-done.9 = bf16[1024,256]{1,0:T(8,128)(2,1)S(1)} collective-permute-done((bf16[1024,256]{1,0:T(8,128)(2,1)S(1)}, bf16[1024,256]{1,0:T(8,128)(2,1)S(1)}, u32[]{:S(2)}, u32[]{:S(2)}) %collective-permute-start.9) | collective-permute-done | bytes 524320 | tf_op jit(solution)/shard_map/ppermute | solution.py:20
  382.3 17.3 %collective-permute-done.11 = bf16[1024,256]{1,0:T(8,128)(2,1)S(1)} collective-permute-done((bf16[1024,256]{1,0:T(8,128)(2,1)S(1)}, bf16[1024,256]{1,0:T(8,128)(2,1)S(1)}, u32[]{:S(2)}, u32[]{:S(2)}) %collective-permute-start.11) | collective-permute-done | bytes 524320 | tf_op jit(solution)/shard_map/ppermute | solution.py:20
  460.4 133.6 %reduce-scatter.14.cloned.1.call-done = f32[1024,256]{1,0:T(8,128)} async-done(((f32[1024,2048]{1,0:T(8,128)}), f32[1024,256]{1,0:T(8,128)}) %reduce-scatter.14.cloned.1.call-update) | async-done | bytes 1048592 | tf_op jit(solution)/shard_map/reduce_scatter | solution.py:175
  606.3 18.9 %collective-permute-done.14 = bf16[1024,256]{1,0:T(8,128)(2,1)S(1)} collective-permute-done((bf16[1024,256]{1,0:T(8,128)(2,1)S(1)}, bf16[1024,256]{1,0:T(8,128)(2,1)S(1)}, u32[]{:S(2)}, u32[]{:S(2)}) %collective-permute-start.14) | collective-permute-done | bytes 524320 | tf_op jit(solution)/shard_map/ppermute | solution.py:20
  629.9 19.4 %collective-permute-done.16 = bf16[1024,256]{1,0:T(8,128)(2,1)S(1)} collective-permute-done((bf16[1024,256]{1,0:T(8,128)(2,1)S(1)}, bf16[1024,256]{1,0:T(8,128)(2,1)S(1)}, u32[]{:S(2)}, u32[]{:S(2)}) %collective-permute-start.16) | collective-permute-done | bytes 524320 | tf_op jit(solution)/shard_map/ppermute | solution.py:20
  654.7 18.7 %collective-permute-done.18 = bf16[1024,256]{1,0:T(8,128)(2,1)S(1)} collective-permute-done((bf16[1024,256]{1,0:T(8,128)(2,1)S(1)}, bf16[1024,256]{1,0:T(8,128)(2,1)S(1)}, u32[]{:S(2)}, u32[]{:S(2)}) %collective-permute-start.18) | collective-permute-done | bytes 524320 | tf_op jit(solution)/shard_map/ppermute | solution.py:20
  712.6 145.4 %reduce-scatter.16.cloned.1.call-done = f32[1024,256]{1,0:T(8,128)} async-done(((f32[1024,2048]{1,0:T(8,128)}), f32[1024,256]{1,0:T(8,128)}) %reduce-scatter.16.cloned.1.call-update) | async-done | bytes 1048592 | tf_op jit(solution)/shard_map/reduce_scatter | solution.py:191
  859.9 19.7 %all-reduce.1 = (f32[1024]{0:T(1024)S(1)}, f32[1024]{0:T(1024)S(1)}) all-reduce(f32[1024]{0:T(1024)S(1)} %get-tuple-element.326, f32[1024]{0:T(1024)S(1)} %get-tuple-element.325), channel_id=1, replica_groups=mesh['dp'=4,'wide'=8] {'wide'}, use_global_device_ids=true, to_apply=%region_26.27 | all-reduce | flops 2048 | bytes 16384 | tf_op jit(solution)/shard_map/psum | solution.py:167
  915.2 18.2 %collective-permute-done.23 = bf16[1024,256]{1,0:T(8,128)(2,1)} collective-permute-done((bf16[1024,256]{1,0:T(8,128)(2,1)S(1)}, bf16[1024,256]{1,0:T(8,128)(2,1)}, u32[]{:S(2)}, u32[]{:S(2)}) %collective-permute-start.23) | collective-permute-done | bytes 524320 | tf_op jit(solution)/shard_map/ppermute | solution.py:20
  975.9 30.4 %while.54 = (s32[]{:T(128)}, f32[1024,2,128]{0,2,1:T(8,128)S(1)}, f32[1024,2,128]{0,2,1:T(8,128)}, f32[2,512,2,128]{3,1,2,0:T(8,128)}, s32[2]{0:T(128)S(1)}, /*i...) while((s32[]{:T(128)}, f32[1024,2,128]{0,2,1:T(8,128)S(1)}, ...), condition=%wide.region_31.32_spmd.clone.clone, body=%wide.region_29.31_spmd.clone.sunk.clone | while | flops 1357250560 | bytes 90224648 | solution.py:160
  1091.7 74.4 %reduce-scatter.18.cloned.1.call-done = f32[1024,256]{1,0:T(8,128)} async-done(((f32[1024,2048]{1,0:T(8,128)}), f32[1024,256]{1,0:T(8,128)}) %reduce-scatter.18.cloned.1.call-update) | async-done | bytes 1048592 | tf_op jit(solution)/shard_map/reduce_scatter | solution.py:191
  1167.9 19.7 %all-reduce = (f32[1024]{0:T(1024)S(1)}, f32[1024]{0:T(1024)S(1)}) all-reduce(f32[1024]{0:T(1024)S(1)} %get-tuple-element.324, f32[1024]{0:T(1024)S(1)} %get-tuple-element.323), channel_id=1, replica_groups=mesh['dp'=4,'wide'=8] {'wide'}, use_global_device_ids=true, to_apply=%region_36.37 | all-reduce | flops 2048 | bytes 16384 | tf_op jit(solution)/shard_map/psum | solution.py:167
  1197.0 38.0 %psum.71 = f32[2,4,6]{2,1,0:T(4,128)} all-reduce(f32[2,4,6]{2,1,0:T(4,128)S(1)} %pad_maximum_fusion.3), channel_id=1, replica_groups=mesh['dp'=4,'wide'=8] {'dp','wide'}, use_global_device_ids=true, to_apply=%region_50.51 | all-reduce | flops 48 | bytes 384 | tf_op jit(solution)/shard_map/psum | solution.py:346
  1240.8 74.6 %reduce-scatter.28.cloned.1.call-done = f32[512,1024]{1,0:T(8,128)} async-done(((f32[2048,1024]{1,0:T(8,128)}), f32[512,1024]{1,0:T(8,128)}) %reduce-scatter.28.cloned.1.call-update) | async-done | bytes 2097168 | tf_op jit(solution)/shard_map/reduce_scatter | solution.py:280
  1315.4 74.4 %reduce-scatter.30.cloned.1.call-done = f32[512,1024]{1,0:T(8,128)} async-done(((f32[2048,1024]{1,0:T(8,128)}), f32[512,1024]{1,0:T(8,128)}) %reduce-scatter.30.cloned.1.call-update) | async-done | bytes 2097168 | tf_op jit(solution)/shard_map/reduce_scatter | solution.py:281
  1389.8 34.2 %reduce-scatter.26.cloned.1.call-done = f32[256,512]{1,0:T(8,128)} async-done(((f32[256,2048]{1,0:T(8,128)}), f32[256,512]{1,0:T(8,128)}) %reduce-scatter.26.cloned.1.call-update) | async-done | bytes 524304 | tf_op jit(solution)/shard_map/reduce_scatter | solution.py:359
  1424.0 34.1 %reduce-scatter.24.cloned.1.call-done = f32[512,256]{1,0:T(8,128)} async-done(((f32[2048,256]{1,0:T(8,128)}), f32[512,256]{1,0:T(8,128)}) %reduce-scatter.24.cloned.1.call-update) | async-done | bytes 524304 | tf_op jit(solution)/shard_map/reduce_scatter | solution.py:358
  1458.1 34.1 %reduce-scatter.22.cloned.1.call-done = f32[512,256]{1,0:T(8,128)} async-done(((f32[2048,256]{1,0:T(8,128)}), f32[512,256]{1,0:T(8,128)}) %reduce-scatter.22.cloned.1.call-update) | async-done | bytes 524304 | tf_op jit(solution)/shard_map/reduce_scatter | solution.py:357
  1492.3 34.1 %reduce-scatter.20.cloned.1.call-done = f32[512,256]{1,0:T(8,128)} async-done(((f32[2048,256]{1,0:T(8,128)}), f32[512,256]{1,0:T(8,128)}) %reduce-scatter.20.cloned.1.call-update) | async-done | bytes 524304 | tf_op jit(solution)/shard_map/reduce_scatter | solution.py:356
  (400 shorter events, 491.0 us)
Async XLA Ops:
  7.2 116.2 %all-gather.10.cloned.1.call-start = ((), (), s32[]{:S(2)}) async-start(), calls=%async_computation.12 | async-start | bytes 1310720 | tf_op jit(solution)/shard_map/all_gather | solution.py:225
  7.9 120.3 %all-gather.8.cloned.1.call-start = ((), (), s32[]{:S(2)}) async-start(), calls=%async_computation.11 | async-start | bytes 1310720 | tf_op jit(solution)/shard_map/all_gather | solution.py:224
  8.7 124.8 %all-gather.12.cloned.1.call-start = ((), (), s32[]{:S(2)}) async-start(), calls=%async_computation.13 | async-start | bytes 1310720 | tf_op jit(solution)/shard_map/all_gather | solution.py:226
  9.4 142.5 %all-gather.14.cloned.1.call-start = ((), (), s32[]{:S(2)}) async-start(), calls=%async_computation.14 | async-start | bytes 1310720 | tf_op jit(solution)/shard_map/all_gather | solution.py:227
  45.3 257.8 %reduce-scatter.12.cloned.1.call-start = ((), (), s32[]{:S(2)}) async-start(), calls=%async_computation.15 | async-start | bytes 9437184 | tf_op jit(solution)/shard_map/reduce_scatter | solution.py:175
  88.4 27.6 %collective-permute-start.5 = (bf16[1024,256]{1,0:T(8,128)(2,1)}, bf16[1024,256]{1,0:T(8,128)(2,1)S(1)}, u32[]{:S(2)}, u32[]{:S(2)}) collective-permute-start(bf16[1024,256]{1,0:T(8,128)(2,1)} %collective-permute-done.3), channel_id=1, source_target_pairs={{0,7},{1,0},{2,1},{3,2},{4,3},{5,4},{6,5},{7,6},{8,15},{9,8},{10,9... | collective-permute-start | bytes 1572872 | tf_op jit(solution)/shard_map/ppermute | solution.py:23
  157.9 258.2 %all-gather.16.cloned.1.call-start = ((), (), s32[]{:S(2)}) async-start(), calls=%async_computation.16 | async-start | bytes 5242880 | tf_op jit(solution)/shard_map/all_gather | solution.py:230
  158.4 267.6 %all-gather.18.cloned.1.call-start = ((), (), s32[]{:S(2)}) async-start(), calls=%async_computation.17 | async-start | bytes 5242880 | tf_op jit(solution)/shard_map/all_gather | solution.py:231
  159.2 279.0 %all-gather.20.cloned.1.call-start = ((), (), s32[]{:S(2)}) async-start(), calls=%async_computation.18 | async-start | bytes 5242880 | tf_op jit(solution)/shard_map/all_gather | solution.py:232
  159.9 434.0 %reduce-scatter.14.cloned.1.call-start = ((), (), s32[]{:S(2)}) async-start(), calls=%async_computation.19 | async-start | bytes 9437184 | tf_op jit(solution)/shard_map/reduce_scatter | solution.py:175
  377.9 27.5 %collective-permute-start.12 = (bf16[1024,256]{1,0:T(8,128)(2,1)S(1)}, bf16[1024,256]{1,0:T(8,128)(2,1)S(1)}, u32[]{:S(2)}, u32[]{:S(2)}) collective-permute-start(bf16[1024,256]{1,0:T(8,128)(2,1)S(1)} %collective-permute-done.10), channel_id=1, source_target_pairs={{0,7},{1,0},{2,1},{3,2},{4,3},{5,4},{6,5},{7,6},{8,15},{9,8},{10,9... | collective-permute-start | bytes 1572872 | tf_op jit(solution)/shard_map/ppermute | solution.py:23
  448.8 409.3 %reduce-scatter.16.cloned.1.call-start = ((), (), s32[]{:S(2)}) async-start(), calls=%async_computation.20 | async-start | bytes 9437184 | tf_op jit(solution)/shard_map/reduce_scatter | solution.py:191
  603.0 24.6 %collective-permute-start.15 = (bf16[1024,256]{1,0:T(8,128)(2,1)S(1)}, bf16[1024,256]{1,0:T(8,128)(2,1)S(1)}, u32[]{:S(2)}, u32[]{:S(2)}) collective-permute-start(bf16[1024,256]{1,0:T(8,128)(2,1)S(1)} %get-tuple-element.319), channel_id=1, source_target_pairs={{0,7},{1,0},{2,1},{3,2},{4,3},{5,4},{6,5},{7,6},{8,15},{9,8},{10,9... | collective-permute-start | bytes 1572872 | tf_op jit(solution)/shard_map/ppermute | solution.py:23
  627.6 24.7 %collective-permute-start.17 = (bf16[1024,256]{1,0:T(8,128)(2,1)S(1)}, bf16[1024,256]{1,0:T(8,128)(2,1)S(1)}, u32[]{:S(2)}, u32[]{:S(2)}) collective-permute-start(bf16[1024,256]{1,0:T(8,128)(2,1)S(1)} %collective-permute-done.15), channel_id=1, source_target_pairs={{0,7},{1,0},{2,1},{3,2},{4,3},{5,4},{6,5},{7,6},{8,15},{9,8},{10,9... | collective-permute-start | bytes 1572872 | tf_op jit(solution)/shard_map/ppermute | solution.py:23
  712.6 453.4 %reduce-scatter.18.cloned.1.call-start = ((), (), s32[]{:S(2)}) async-start(), calls=%async_computation.21 | async-start | bytes 9437184 | tf_op jit(solution)/shard_map/reduce_scatter | solution.py:191
  908.8 24.6 %collective-permute-start.23 = (bf16[1024,256]{1,0:T(8,128)(2,1)S(1)}, bf16[1024,256]{1,0:T(8,128)(2,1)}, u32[]{:S(2)}, u32[]{:S(2)}) collective-permute-start(bf16[1024,256]{1,0:T(8,128)(2,1)S(1)} %collective-permute-done.21), channel_id=1, source_target_pairs={{0,1},{1,2},{2,3},{3,4},{4,5},{5,6},{6,7},{7,0},{8,9},{9,10},{10,1... | collective-permute-start | bytes 1572872 | tf_op jit(solution)/shard_map/ppermute | solution.py:20
  911.3 29.2 %collective-permute-start.24 = (bf16[1024,256]{1,0:T(8,128)(2,1)}, bf16[1024,256]{1,0:T(8,128)(2,1)}, u32[]{:S(2)}, u32[]{:S(2)}) collective-permute-start(bf16[1024,256]{1,0:T(8,128)(2,1)} %collective-permute-done.22), channel_id=1, source_target_pairs={{0,7},{1,0},{2,1},{3,2},{4,3},{5,4},{6,5},{7,6},{8,15},{9,8},{10,9... | collective-permute-start | bytes 1572872 | tf_op jit(solution)/shard_map/ppermute | solution.py:23
  1020.8 220.0 %reduce-scatter.32.cloned.1.call-start = ((), (), s32[]{:S(2)}) async-start(), calls=%async_computation.28 | async-start | bytes 10485760 | tf_op jit(solution)/shard_map/reduce_scatter | solution.py:282
  1031.8 283.6 %reduce-scatter.28.cloned.1.call-start = ((), (), s32[]{:S(2)}) async-start(), calls=%async_computation.26 | async-start | bytes 10485760 | tf_op jit(solution)/shard_map/reduce_scatter | solution.py:280
  1042.5 347.3 %reduce-scatter.30.cloned.1.call-start = ((), (), s32[]{:S(2)}) async-start(), calls=%async_computation.27 | async-start | bytes 10485760 | tf_op jit(solution)/shard_map/reduce_scatter | solution.py:281
  1053.6 370.3 %reduce-scatter.26.cloned.1.call-start = ((), (), s32[]{:S(2)}) async-start(), calls=%async_computation.25 | async-start | bytes 2621440 | tf_op jit(solution)/shard_map/reduce_scatter | solution.py:359
  1059.7 398.4 %reduce-scatter.24.cloned.1.call-start = ((), (), s32[]{:S(2)}) async-start(), calls=%async_computation.24 | async-start | bytes 2621440 | tf_op jit(solution)/shard_map/reduce_scatter | solution.py:358
  1064.9 427.4 %reduce-scatter.22.cloned.1.call-start = ((), (), s32[]{:S(2)}) async-start(), calls=%async_computation.23 | async-start | bytes 2621440 | tf_op jit(solution)/shard_map/reduce_scatter | solution.py:357
  1069.9 456.5 %reduce-scatter.20.cloned.1.call-start = ((), (), s32[]{:S(2)}) async-start(), calls=%async_computation.22 | async-start | bytes 2621440 | tf_op jit(solution)/shard_map/reduce_scatter | solution.py:356
  (91 other events, 1597.4 us)
Sparse Core Ops, SparseCore 0:
  9.5 19.4 all-gather.9
  30.6 16.6 all-gather.7
  48.9 16.6 all-gather.11
  67.0 16.6 all-gather.13
  158.0 145.0 reduce-scatter.11
  304.5 33.5 all-gather.15
  339.7 34.4 all-gather.17
  375.7 34.4 all-gather.19
  448.9 145.0 reduce-scatter.13
  712.7 145.2 reduce-scatter.15
  1021.0 145.0 reduce-scatter.17
  1169.0 71.7 reduce-scatter.31
  1244.0 71.3 reduce-scatter.27
  1318.4 71.3 reduce-scatter.29
  1392.8 31.1 reduce-scatter.25
  1426.9 31.1 reduce-scatter.23
  1461.1 31.1 reduce-scatter.21
  1495.2 31.1 reduce-scatter.19
